TPU v7x, 32 devices: a 4x4x1 block of a 4x4x8 slice. The times are simulated.
32 devices in a mesh: dp: 1 (over z), tp: 32 (over y, x, core).
Axes of the slice: x: 4, y: 4, z: 1, core: 2. Of those that a mesh axis runs over, the one named last changes fastest.
The devices are a block of a 4x4x8 slice.
Arguments:
- x_seq: bfloat16 [1, 4096, 6144], P('dp', 'tp')
- ln_gain: float32 [6144], replicated
- ln_bias: float32 [6144], replicated
- w_qkv: bfloat16 [6144, 64, 3, 96], P(None, 'tp')
- w_out: bfloat16 [6144, 6144], P('tp')
- w_up: bfloat16 [6144, 24576], P(None, 'tp')
- w_down: bfloat16 [24576, 6144], P('tp')
Outputs:
- output: bfloat16 [1, 4096, 6144], P('dp', 'tp')
All inputs are finite; a program needn't handle non-finite values.
Results may differ from a plain program's by a relative error of at most 0.0126939.
Values are sent between devices in bfloat16 or wider.
A program may use at most 768 MiB of HBM per device.

v0:
```python
import jax
import jax.numpy as jnp
from jax import lax
from jax.sharding import PartitionSpec as P, NamedSharding

LN_EPS = 1e-5


def layer_norm(x_f32, ln_gain, ln_bias):
    row_mean = jnp.mean(x_f32, axis=-1, keepdims=True)
    centered = x_f32 - row_mean
    variance = jnp.mean(centered * centered, axis=-1, keepdims=True)
    return centered * lax.rsqrt(variance + LN_EPS) * ln_gain + ln_bias


def solution(mesh):
    def local_layer(x_blk, ln_gain, ln_bias, w_qkv, w_out, w_up, w_down):
        x_full = lax.all_gather(x_blk, "tp", axis=1, tiled=True)
        seq_len = x_full.shape[1]
        model_dim = x_full.shape[2]
        kv_local, group_width, head_dim = w_qkv.shape[1:]
        group_q = group_width - 2
        normed = layer_norm(x_full.astype(jnp.float32), ln_gain, ln_bias).astype(jnp.bfloat16)
        proj_qkv = jnp.einsum("bsd,dgjh->bsgjh", normed, w_qkv,
                              preferred_element_type=jnp.float32).astype(jnp.bfloat16)
        queries = proj_qkv[:, :, :, :group_q]
        key_rows = proj_qkv[:, :, :, group_q]
        value_rows = proj_qkv[:, :, :, group_q + 1]
        scores = jnp.einsum("bsgjh,btgh->bgjst", queries, key_rows,
                            preferred_element_type=jnp.float32) * (head_dim ** -0.5)
        causal = (lax.broadcasted_iota(jnp.int32, (seq_len, seq_len), 0)
                  >= lax.broadcasted_iota(jnp.int32, (seq_len, seq_len), 1))
        scores = jnp.where(causal, scores, -jnp.inf)
        attn_prob = jax.nn.softmax(scores, axis=-1).astype(jnp.bfloat16)
        context = jnp.einsum("bgjst,btgh->bgjsh", attn_prob, value_rows,
                             preferred_element_type=jnp.float32).astype(jnp.bfloat16)
        w_heads = w_out.reshape(kv_local, group_q, head_dim, model_dim)
        attn_part = jnp.einsum("bgjsh,gjhd->bsd", context, w_heads, preferred_element_type=jnp.float32)
        hidden = jnp.einsum("bsd,df->bsf", normed, w_up, preferred_element_type=jnp.float32)
        activated = jax.nn.gelu(hidden, approximate=False).astype(jnp.bfloat16)
        mlp_part = jnp.einsum("bsf,fd->bsd", activated, w_down, preferred_element_type=jnp.float32)
        branch_part = (attn_part + mlp_part).astype(jnp.bfloat16)
        branch = lax.psum_scatter(branch_part, "tp", scatter_dimension=1, tiled=True)
        return (x_blk.astype(jnp.float32) + branch.astype(jnp.float32)).astype(jnp.bfloat16)

    return jax.shard_map(
        local_layer, mesh=mesh,
        in_specs=(P("dp", "tp", None), P(), P(), P(None, "tp", None, None),
                  P("tp", None), P(None, "tp"), P("tp", None)),
        out_specs=P("dp", "tp", None), check_vma=False)
```

profile of v0, /device:TPU:97, one launch (start us, length us, event | category | flops | bytes accessed | tf_op | source)
XLA Modules:
  0.0 798.7 jit_solution(11421503788300292543)
XLA Ops:
  6.5 0.0 copy-start
  6.6 0.0 all-gather.2.cloned.1.call-start
  6.6 0.7 all-gather.2.cloned.1.call-update
  7.3 0.1 reduce-scatter.2.cloned.1.call-start
  7.4 11.0 %iota_compare_fusion = pred[4096,4096]{0,1:T(8,128)(4,1)} fusion(), kind=kLoop, calls=%fused_computation.17 | loop fusion | flops 16777216 | bytes 16777216 | tf_op jit(solution)/shard_map/ge | solution.py:31
  18.4 147.5 %all-gather.2.cloned.1.call-done = bf16[1,4096,6144]{2,1,0:T(8,128)(2,1)} async-done(((bf16[1,128,6144]{2,1,0:T(8,128)(2,1)}), bf16[1,4096,6144]{2,1,0:T(8,128)(2,1)}) %all-gather.2.cloned.1.call-update) | async-done | bytes 50331664 | tf_op jit(solution)/shard_map/all_gather | solution.py:18
  165.9 16.1 %convert_reduce_fusion = f32[4096]{0:T(1024)S(1)} fusion(bf16[1,4096,6144]{2,1,0:T(8,128)(2,1)} %all-gather.2.cloned.1.call-done), kind=kLoop, calls=%fused_computation.4 | loop fusion | flops 50327552 | bytes 50348032 | tf_op jit(solution)/shard_map/reduce_sum | solution.py:10
  182.0 0.0 copy-start.1
  182.0 0.0 copy-start.5
  182.0 0.0 copy-start.7
  182.1 19.9 %fusion.4 = f32[4096]{0:T(1024)S(1)} fusion(bf16[1,4096,6144]{2,1,0:T(8,128)(2,1)} %all-gather.2.cloned.1.call-done, f32[4096]{0:T(1024)S(1)} %broadcast_multiply_fusion), kind=kLoop, calls=%fused_computation.9 | loop fusion | flops 100659200 | bytes 50364416 | tf_op jit(solution)/shard_map/reduce_sum | solution.py:12
  202.0 0.0 copy-start.3
  202.0 0.0 copy-done.1
  202.0 0.0 copy-done.5
  202.0 0.0 copy-done.7
  202.0 38.9 %fusion.97 = f32[4096,576]{0,1} fusion(bf16[6144,576]{0,1:T(8,128)(2,1)} %bitcast.100, bf16[1,4096,6144]{2,1,0:T(8,128)(2,1)} %all-gather.2.cloned.1.call-done, f32[6144]{0:T(1024)S(1)} %copy-done.5, f32[6144]{0:T(1024)S(1)} %copy-done.7, f32[4096]{0:T(1024)S(1)} %add_rsqrt_fusion, f32[4096]{0:T(1024)S(1)} %broadcast_multiply_fusion), kind=kOutput, calls=%fused_computation.112 | convolution fusion | flops 29142024192 | bytes 66928640
  240.9 0.0 copy-done.3
  240.9 6.5 convert_bitcast_fusion
  247.4 54.5 %fusion.3 = (f32[2,4096]{1,0:T(2,128)S(1)}, f32[2,4096,4096]{2,1,0:T(8,128)}) fusion(pred[4096,4096]{0,1:T(8,128)(4,1)} %iota_compare_fusion, bf16[1,4096,2,3,96]{1,4,3,2,0:T(8,128)(2,1)} %convert_bitcast_fusion), kind=kOutput, calls=%fused_computation.8 | convolution fusion | flops 6543106048 | bytes 154173440 | tf_op jit(solution)/shard_map/bsgjh,btgh->bgjst/dot_general | solution.py:29
  302.0 46.2 %fusion.2 = f32[2,4096]{1,0:T(2,128)S(1)} fusion(f32[2,4096,4096]{2,1,0:T(8,128)} %get-tuple-element.6, f32[2,4096]{1,0:T(2,128)S(1)} %get-tuple-element.5, pred[4096,4096]{0,1:T(8,128)(4,1)} %iota_compare_fusion), kind=kLoop, calls=%fused_computation.7 | loop fusion | flops 134209536 | bytes 151060480 | tf_op jit(solution)/shard_map/reduce_sum | solution.py:34
  348.2 53.7 %fusion.54.clone.4 = bf16[2,4096,96]{1,2,0:T(8,128)(2,1)} fusion(f32[2,4096]{1,0:T(2,128)S(1)} %fusion.2, f32[2,4096]{1,0:T(2,128)S(1)} %get-tuple-element.5, f32[2,4096,4096]{2,1,0:T(8,128)} %get-tuple-element.6, pred[4096,4096]{0,1:T(8,128)(4,1)} %iota_compare_fusion, bf16[1,4096,2,3,96]{1,4,3,2,0:T(8,128)(2,1)} %convert_bitcast_fusion), kind=kOutput, calls=%fused_computation.69.clone.clone.clone.1 | convolution fusion | flops 6611009536 | bytes 154206208 | tf_op jit(solution)/shard_map/bgjst,btgh->bgjsh/dot_general | solution.py:35
  401.9 0.0 copy-done
  401.9 0.0 copy-start.2
  401.9 0.0 copy-start.4
  402.0 0.0 copy-start.6
  402.0 0.0 copy-start.8
  402.0 35.9 %fusion.58 = f32[4096,6144,1]{1,0,2:T(8,128)} fusion(bf16[2,96,6144]{2,1,0:T(8,128)(2,1)S(1)} %bitcast.98, bf16[2,4096,96]{1,2,0:T(8,128)(2,1)} %fusion.54.clone.4), kind=kOutput, calls=%fused_computation.70 | convolution fusion | flops 9663676416 | bytes 104595456 | tf_op jit(solution)/shard_map/bgjsh,gjhd->bsd/dot_general | solution.py:38
  437.9 0.0 copy-done.2
  437.9 0.0 copy-done.4
  437.9 0.0 copy-done.6
  437.9 0.0 copy-done.8
  437.9 78.4 %fusion.119 = bf16[4096,768]{1,0:T(8,128)(2,1)} fusion(bf16[6144,768]{1,0:T(8,128)(2,1)} %param.12, bf16[1,4096,6144]{2,1,0:T(8,128)(2,1)} %all-gather.2.cloned.1.call-done, f32[6144]{0:T(1024)S(1)} %copy-done.6, f32[6144]{0:T(1024)S(1)} %copy-done.8, f32[4096]{0:T(1024)S(1)} %copy-done.4, f32[4096]{0:T(1024)S(1)} %copy-done.2), kind=kOutput, calls=%fused_computation.23.clone.clone.1 | convolution fusion | flops 39010172928 | bytes 66142208 | tf_op jit(solution)/shard_map/bsd,df->bsf/dot_general | solution.py:39
  516.3 63.4 %fusion.12 = bf16[1,4096,6144]{2,1,0:T(8,128)(2,1)} fusion(bf16[768,6144]{1,0:T(8,128)(2,1)} %param.13, f32[4096,6144,1]{1,0,2:T(8,128)} %fusion.58, bf16[4096,768]{1,0:T(8,128)(2,1)} %fusion.119), kind=kOutput, calls=%fused_computation.19 | convolution fusion | flops 38705037312 | bytes 166723584 | tf_op jit(solution)/shard_map/bsf,fd->bsd/dot_general | solution.py:41
  579.7 0.1 reduce-scatter.2.cloned.1.call-update
  579.8 208.2 %reduce-scatter.2.cloned.1.call-done = bf16[1,128,6144]{2,1,0:T(8,128)(2,1)} async-done(((bf16[1,4096,6144]{2,1,0:T(8,128)(2,1)}), bf16[1,128,6144]{2,1,0:T(8,128)(2,1)}) %reduce-scatter.2.cloned.1.call-update) | async-done | bytes 1572880 | tf_op jit(solution)/shard_map/reduce_scatter | solution.py:43
  788.0 3.4 add_convert_fusion
  (2 shorter events, 0.0 us)
Async XLA Ops:
  6.5 395.4 %copy-start = (bf16[192,6144]{1,0:T(8,128)(2,1)S(1)}, bf16[192,6144]{1,0:T(8,128)(2,1)}, u32[]{:S(2)}) copy-start(bf16[192,6144]{1,0:T(8,128)(2,1)} %param.11) | copy-start | bytes 7077892
  6.6 159.4 %all-gather.2.cloned.1.call-start = ((), (), s32[]{:S(2)}) async-start(), calls=%async_computation.1 | async-start | bytes 51904512 | tf_op jit(solution)/shard_map/all_gather | solution.py:18
  7.3 780.7 %reduce-scatter.2.cloned.1.call-start = ((), (), s32[]{:S(2)}) async-start(), calls=%async_computation.2 | async-start | bytes 51904512 | tf_op jit(solution)/shard_map/reduce_scatter | solution.py:43
  182.0 20.0 %copy-start.1 = (f32[4096]{0:T(1024)}, f32[4096]{0:T(1024)S(1)}, u32[]{:S(2)}) copy-start(f32[4096]{0:T(1024)S(1)} %broadcast_multiply_fusion) | copy-start | bytes 49156
  182.0 20.0 %copy-start.5 = (f32[6144]{0:T(1024)S(1)}, f32[6144]{0:T(1024)}, u32[]{:S(2)}) copy-start(f32[6144]{0:T(1024)} %param.9) | copy-start | bytes 73732
  182.0 20.0 %copy-start.7 = (f32[6144]{0:T(1024)S(1)}, f32[6144]{0:T(1024)}, u32[]{:S(2)}) copy-start(f32[6144]{0:T(1024)} %param.8) | copy-start | bytes 73732
  202.0 38.9 %copy-start.3 = (f32[4096]{0:T(1024)}, f32[4096]{0:T(1024)S(1)}, u32[]{:S(2)}) copy-start(f32[4096]{0:T(1024)S(1)} %add_rsqrt_fusion) | copy-start | bytes 49156
  401.9 36.0 %copy-start.2 = (f32[4096]{0:T(1024)S(1)}, f32[4096]{0:T(1024)}, u32[]{:S(2)}) copy-start(f32[4096]{0:T(1024)} %copy-done.1) | copy-start | bytes 49156
  401.9 36.0 %copy-start.4 = (f32[4096]{0:T(1024)S(1)}, f32[4096]{0:T(1024)}, u32[]{:S(2)}) copy-start(f32[4096]{0:T(1024)} %copy-done.3) | copy-start | bytes 49156
  402.0 36.0 %copy-start.6 = (f32[6144]{0:T(1024)S(1)}, f32[6144]{0:T(1024)}, u32[]{:S(2)}) copy-start(f32[6144]{0:T(1024)} %param.9) | copy-start | bytes 73732
  402.0 36.0 %copy-start.8 = (f32[6144]{0:T(1024)S(1)}, f32[6144]{0:T(1024)}, u32[]{:S(2)}) copy-start(f32[6144]{0:T(1024)} %param.8) | copy-start | bytes 73732
Sparse Core Ops, SparseCore 0:
  9.4 156.4 all-gather.1
  579.9 208.0 reduce-scatter.1
where the time goes:
time: 811 us; the launch traced here: 799 us
  waiting for transfers between devices  357 us (44%)
  matrix products  325 us (40%)
  other arithmetic  103 us (13%)
  between operations  14 us (2%)
    reduce_scatter x1, waiting for transfers between devices, local_layer(): lax.psum_scatter(branch_part, 'tp', scatter_dimension=1, tiled=True)  208 us
    all_gather x1, waiting for transfers between devices, local_layer(): x_full = lax.all_gather(x_blk, 'tp', axis=1, tiled=True)  148 us
    dot_general x1, matrix products, local_layer(): jnp.einsum('bsd,df->bsf', normed, w_up, preferred_element_type=jnp.float32)  78.4 us
    dot_general x1, matrix products, local_layer(): jnp.einsum('bsf,fd->bsd', activated, w_down, preferred_element_type=jnp.f...  63.4 us
    dot_general x1, matrix products, local_layer(): jnp.einsum('bsgjh,btgh->bgjst', queries, key_rows, preferred_element_type...  54.5 us
    dot_general x1, matrix products, local_layer(): jnp.einsum('bgjst,btgh->bgjsh', attn_prob, value_rows, preferred_element_...  53.7 us
    reduce_sum x1, other arithmetic, local_layer(): attn_prob = jax.nn.softmax(scores, axis=-1).astype(jnp.bfloat16)  46.2 us
    unnamed x1, matrix products  38.9 us
  transfers between devices with their start and end apart: 2, of which 2 were waited for; matrix products, arithmetic and copies ran while one was open for 1% of the time, Pallas kernels for 0%

commit v1 on v0

v1 whole, which is shorter than its diff:
```python
import functools

import jax
import jax.numpy as jnp
from jax import lax
from jax.experimental import pallas as pl
from jax.experimental.pallas import tpu as pltpu
from jax.sharding import PartitionSpec as P

OFFSETS = {"o": 0, "p": 1, "m": -1, "t": 2}


def decode(text, size):
    events = []
    for n in range(0, len(text), size):
        kind, i, j = text[n:n + 3]
        half = text[n + 3:n + size]
        events.append((kind, OFFSETS[i], OFFSETS[j]) + ((int(half),) if half.isdigit() else ()))
    return events


STEPS = [e[1:] for e in decode("-oo-op-om-po-mo-ot-to-pp-mp-pm-mm-pt-tp-mt-tm-tt", 3)]
BEFORE = [
    "aoo0aoo1loo-",
    "aop0aom0apo0amo0aop1aom1apo1amo1lop-lom-",
    "",
    "ato1",
    "",
    "lto-",
    "app1apm1",
    "lpp-",
    "amp1amm1lmp-",
    "atp0atm0lpm-lmm-",
    "atp1atm1",
    "apt0apt1lpt-",
    "ltp-amt0amt1lmt-",
    "ltm-",
    "att0att1",
    "ltt-",
]
BEFORE = [decode(text, 4) for text in BEFORE]
BETWEEN = [
    "",
    "lpo-",
    "apm0aot0ato0lmo-",
    "app0amm0",
    "aot1amp0lot-",
    "",
    "",
    "",
    "",
    "",
    "",
    "",
    "",
    "",
    "",
    "",
]
BETWEEN = [decode(text, 4) for text in BETWEEN]
EARLY = [e[1:] for e in decode("-oo-op-om-po-mo", 3)]
ORDER2 = [e[1:] for e in decode("-tt-tp-pt-tm-mt-pp-mm-pm-mp-ot-to-po-op-mo-om-oo", 3)]
EVENTS2 = [
    "",
    "",
    "Att",
    "Apt",
    "AtpLtp",
    "BtpAmt",
    "AtmLtm",
    "BtmAppLpp",
    "BppAmmLmm",
    "BmmAmpLmp",
    "BmpApmLpm",
    "BpmAtoLto",
    "BtoAot",
    "Aop",
    "Apo",
    "Aom",
    "LpoAmoLopBpoLmoBopAooBmoLomBomLooBoo",
]
EVENTS2 = [decode(text, 3) for text in EVENTS2]
NS = 10
MESH = pl.DeviceIdType.MESH
SIDE = 4
LN_EPS = 1e-5
f32, bf16 = jnp.float32, jnp.bfloat16
KT = 1024
CHUNKS = 3
NEG = -1e30
LOG2E = 1.4426950408889634


class Place:
    def __init__(self):
        self.tp = lax.axis_index("tp")
        self.colour = lax.rem(self.tp, 2)
        chip = lax.div(self.tp, 2)
        self.x, self.y = lax.rem(chip, SIDE), lax.div(chip, SIDE)

    def chip(self, colour, i, j):
        dx = (1 - colour) * i + colour * j
        dy = (1 - colour) * j + colour * i
        return lax.rem(self.y + dy + SIDE, SIDE) * SIDE + lax.rem(self.x + dx + SIDE, SIDE)

    def device(self, i, j):
        return {"tp": self.chip(self.colour, i, j) * 2 + self.colour}

    def partner(self):
        return {"tp": self.tp + 1 - 2 * self.colour}


def greet(place):
    barrier = pltpu.get_barrier_semaphore()
    others = [place.device(1, 0), place.device(-1, 0), place.device(0, 1), place.device(0, -1), place.partner()]
    for other in others:
        pl.semaphore_signal(barrier, inc=1, device_id=other, device_id_type=MESH)
    return lambda: pl.semaphore_wait(barrier, len(others))


def pick(step, values):
    r = jnp.int32(values[0])
    for n, v in enumerate(values[1:], 1):
        r = jnp.where(step == n, jnp.int32(v), r)
    return r


def layer_kernel(x_ref, gain_ref, bias_ref, wqkv_ref, wup_ref, wdown_ref, wout_ref,
                 y_ref, full_ref, act_ref, m_ref, m1_ref, m2_ref,
                 w, qq, kk, vv, lhs, dr, f1, f2, m_sc, l_sc, acc_sc,
                 recv, send, drecv, dsend, ssem, dssem, drsem, m1sem, m2sem, f1sem, f2sem, free, w_sem):
    place = Place()
    me = place.colour
    block, width = x_ref.shape
    half = block // 2
    ffl = wup_ref.shape[1]
    hd2 = wout_ref.shape[0]
    head = hd2 // 2
    pair = 2 * block
    n_steps = len(STEPS)
    ndr = dr.shape[0]
    cw = width // CHUNKS

    wloads = [pltpu.make_async_copy(wdown_ref, w.at[pl.ds(0, ffl)], w_sem.at[0]),
              pltpu.make_async_copy(wout_ref, w.at[pl.ds(ffl, hd2)], w_sem.at[1])]

    def rows_of(colour, i, j, h):
        first = (place.chip(colour, i, j) * 2 + colour) * block + h * half
        return full_ref.at[pl.ds(pl.multiple_of(first, half), half)]

    def chip_rows(ref, i, j):
        return ref.at[pl.ds(pl.multiple_of(place.chip(me, i, j) * pair, pair), pair)]

    def col_chunk(c):
        return pl.ds(pl.multiple_of(c * cw, cw), cw)

    sends = []

    def gather(xs, own, gain, bias, wqkv, wup, tile, acts, mst, in_sem, pw_sem, tile_sem, out_sem, mst_sem):
        loads = [pltpu.make_async_copy(x_ref, xs, in_sem.at[0]),
                 pltpu.make_async_copy(gain_ref, gain, in_sem.at[1]),
                 pltpu.make_async_copy(bias_ref, bias, in_sem.at[2])]
        pwloads = [pltpu.make_async_copy(wqkv_ref, wqkv, pw_sem.at[0]), pltpu.make_async_copy(wup_ref, wup, pw_sem.at[1])]
        for c in loads + pwloads + wloads:
            c.start()
        met = greet(place)
        for c in loads:
            c.wait()

        def norm_rows(start):
            g = gain[...]
            b = bias[...]

            @pl.loop(0, half // 16)
            def _(r):
                rows = pl.ds(pl.multiple_of(start + r * 16, 16), 16)
                v = xs[rows, :].astype(f32)
                mean = jnp.mean(v, axis=-1, keepdims=True)
                cen = v - mean
                var = jnp.mean(cen * cen, axis=-1, keepdims=True)
                own[rows, :] = (cen * lax.rsqrt(var + LN_EPS) * g + b).astype(bf16)

        def source(i, j, h):
            return own.at[pl.ds(h * half, half)] if (i, j) == (0, 0) else rows_of(me, i, j, h)

        def forward(i, j, h, to, ri, rj):
            n = len(sends)
            cp = pltpu.make_async_remote_copy(source(i, j, h), rows_of(me, i, j, h), send.at[n],
                                              recv.at[ri % SIDE, rj % SIDE, h], device_id=place.device(*to), device_id_type=MESH)
            cp.start()
            sends.append((i, j, h))

        def wait_block(colour, i, j, h, sem):
            r = rows_of(colour, i, j, h)
            pltpu.make_async_remote_copy(r, r, send.at[0], sem.at[i % SIDE, j % SIDE, h],
                                         device_id=place.partner(), device_id_type=MESH).wait_recv()

        def arrived(i, j, h):
            if (i, j) != (0, 0):
                wait_block(me, i, j, h, recv)
            if j == 0:
                if i == 0:
                    forward(0, 0, h, (-1, 0), 1, 0)
                    forward(0, 0, h, (1, 0), -1, 0)
                if (i, h) == (1, 0):
                    forward(i, 0, h, (-1, 0), 2, 0)
                if (i, h) == (-1, 1):
                    forward(i, 0, h, (1, 0), 2, 0)
                forward(i, j, h, (0, -1), i, 1)
                forward(i, j, h, (0, 1), i, -1)
            if (j, h) == (1, 0):
                forward(i, j, h, (0, -1), i, 2)
            if (j, h) == (-1, 1):
                forward(i, j, h, (0, 1), i, 2)
            pltpu.make_async_remote_copy(source(i, j, h), rows_of(me, i, j, h), dsend.at[i % SIDE, j % SIDE, h],
                                         drecv.at[i % SIDE, j % SIDE, h], device_id=place.partner(), device_id_type=MESH).start()

        def tile_load(s):
            i, j = STEPS[s]
            if s == 0:
                first = (place.chip(me, 0, 0) * 2 + 1 - me) * block
                return pltpu.make_async_copy(full_ref.at[pl.ds(pl.multiple_of(first, block), block)],
                                             tile.at[0, pl.ds(pl.multiple_of((1 - me) * block, block), block)], tile_sem.at[0])
            return pltpu.make_async_copy(chip_rows(full_ref, i, j), tile.at[s % 2], tile_sem.at[s % 2])

        def act_out(s):
            return pltpu.make_async_copy(acts.at[s % 2], chip_rows(act_ref, *STEPS[s]), out_sem.at[s % 2])

        def m_out(s):
            return [pltpu.make_async_copy(mst.at[c], chip_rows(m_ref, *STEPS[s]).at[:, pl.ds(c * cw, cw)], mst_sem.at[c])
                    for c in range(CHUNKS)]

        def serve(events):
            for e in events:
                if e[0] == "a":
                    arrived(*e[1:])
                else:
                    i, j = e[1:]
                    for h in range(2):
                        wait_block(1 - me, j, i, h, drecv)
                    tile_load(STEPS.index((i, j))).start()

        early = sorted(STEPS.index(c) for c in EARLY)
        norm_rows(0)
        met()
        serve([e for e in BEFORE[0] if e == ("a", 0, 0, 0)])
        norm_rows(half)
        serve([e for e in BEFORE[0] if e == ("a", 0, 0, 1)])
        tile[0, pl.ds(pl.multiple_of(me * block, block), block), :] = own[...]
        for g in range(2):
            qq[pl.ds(g * 128 + head, 128 - head), :] = jnp.zeros((128 - head, qq.shape[1]), bf16)

        @pl.loop(0, n_steps)
        def _(step):
            for s in range(n_steps):
                @pl.when(step == s)
                def _(s=s):
                    serve([e for e in BEFORE[s] if e[1:3] != (0, 0) or e[0] == "l"])
                    if s >= 2 and s - 2 not in early:
                        act_out(s - 2).wait()
                    if s == 0:
                        for c in pwloads:
                            c.wait()
                    tile_load(s).wait()

            p = lax.rem(step, 2)
            b = place.chip(me, pick(step, [i for i, _ in STEPS]), pick(step, [j for _, j in STEPS]))
            at = pl.ds(pl.multiple_of(b * pair, pair), pair)

            @pl.when(step >= 0)
            def _():
                n = tile[p]
                qkv = lax.dot_general(wqkv[...], n, (((1,), (1,)), ((), ())), preferred_element_type=f32)
                for g in range(2):
                    base = g * 3 * head
                    qq[pl.ds(g * 128, head), at] = qkv[base:base + head].astype(bf16)
                    keys = qkv[base + head:base + 2 * head]
                    keys = jnp.concatenate([keys, jnp.zeros((128 - head, pair), f32)], axis=0)
                    kk[at, pl.ds(g * 128, 128)] = keys.T.astype(bf16)
                    vv[pl.ds(g * head, head), at] = qkv[base + 2 * head:base + 3 * head].astype(bf16)
                hid = jnp.dot(n, wup[...], preferred_element_type=f32)
                acts[p] = (0.5 * hid * (1.0 + lax.erf(hid * (0.5 ** 0.5)))).astype(bf16)

            for s in range(n_steps):
                @pl.when(step == s)
                def _(s=s):
                    if s in early:
                        serve(BETWEEN[s])
                        if s == early[0]:
                            for c in wloads:
                                c.wait()
                        else:
                            for c in m_out(early[early.index(s) - 1]):
                                c.wait()
                    else:
                        act_out(s).start()

            if early:
                @pl.when(functools.reduce(jnp.logical_or, [step == s for s in early]))
                def _():
                    @pl.loop(0, CHUNKS)
                    def _(c):
                        mst[c] = jnp.dot(acts[p], w[0:ffl, col_chunk(c)], preferred_element_type=f32).astype(bf16)
                for s in early:
                    @pl.when(step == s)
                    def _(s=s):
                        for c in m_out(s):
                            c.start()

        for s in (n_steps - 2, n_steps - 1):
            if s not in early:
                act_out(s).wait()
        if early:
            for c in m_out(early[-1]):
                c.wait()
        else:
            for c in wloads:
                c.wait()
        for n, (i, j, h) in enumerate(sends):
            if (i, j) == (0, 0):
                pltpu.make_async_remote_copy(source(0, 0, h), rows_of(me, 0, 0, h), send.at[n], recv.at[0, 0, 0],
                                             device_id=place.partner(), device_id_type=MESH).wait_send()
        for h in range(2):
            pltpu.make_async_remote_copy(source(0, 0, h), rows_of(me, 0, 0, h), dsend.at[0, 0, h], recv.at[0, 0, 0],
                                         device_id=place.partner(), device_id_type=MESH).wait_send()

    pl.run_scoped(
        gather, pltpu.VMEM((block, width), bf16), pltpu.VMEM((block, width), bf16), pltpu.VMEM((1, width), f32), pltpu.VMEM((1, width), f32),
        pltpu.VMEM(wqkv_ref.shape, bf16), pltpu.VMEM(wup_ref.shape, bf16), pltpu.VMEM((2, pair, width), bf16),
        pltpu.VMEM((2, pair, ffl), bf16), pltpu.VMEM((CHUNKS, pair, cw), bf16),
        pltpu.SemaphoreType.DMA((3,)), pltpu.SemaphoreType.DMA((2,)), pltpu.SemaphoreType.DMA((2,)), pltpu.SemaphoreType.DMA((2,)),
        pltpu.SemaphoreType.DMA((CHUNKS,)))

    def scatter(xs, pool, stage, x_sem, lq_sem, st_sem):
        pltpu.make_async_copy(x_ref, xs, x_sem).start()

        def unit(s):
            return s % NS

        def hand_unit(s):
            return NS + s % (pool.shape[0] - NS)

        def step_loads(s):
            i, j = ORDER2[s]
            base = place.chip(me, i, j) * pair
            if (i, j) in EARLY:
                res = []
                for n, (colour, u) in enumerate(((me, unit(s)), (1 - me, hand_unit(s)))):
                    at = pl.ds(pl.multiple_of(base + colour * block, block), block)
                    res.append(pltpu.make_async_copy(m_ref.at[at], pool.at[u], lq_sem.at[s % 2, n]))
                return res
            return [pltpu.make_async_copy(chip_rows(act_ref, i, j), lhs.at[s % 2, :, pl.ds(0, ffl)], lq_sem.at[s % 2, 0])]

        def messages(i, j):
            if j == 2:
                return [(0, half, (0, 1), m1_ref.at[i % SIDE, 0], m1sem.at[i % SIDE, 0]),
                        (half, half, (0, -1), m1_ref.at[i % SIDE, 1], m1sem.at[i % SIDE, 1])]
            if j == 1:
                return [(0, block, (0, 1), m2_ref.at[i % SIDE, 0], m2sem.at[i % SIDE, 0])]
            if j == -1:
                return [(0, block, (0, -1), m2_ref.at[i % SIDE, 1], m2sem.at[i % SIDE, 1])]
            if i == 2:
                return [(0, half, (1, 0), f1.at[0], f1sem.at[0]), (half, half, (-1, 0), f1.at[1], f1sem.at[1])]
            if i == 1:
                return [(0, block, (1, 0), f2.at[0], f2sem.at[0])]
            if i == -1:
                return [(0, block, (-1, 0), f2.at[1], f2sem.at[1])]
            return []

        def copies(i, j):
            s = ORDER2.index((i, j))
            return [pltpu.make_async_remote_copy(pool.at[unit(s), pl.ds(r, n)], ref, ssem.at[s, m], sem,
                                                 device_id=place.device(*to), device_id_type=MESH)
                    for m, (r, n, to, ref, sem) in enumerate(messages(i, j))]

        def wait_in(ref, sem):
            pltpu.make_async_remote_copy(ref, ref, ssem.at[0, 0], sem, device_id=place.partner(), device_id_type=MESH).wait_recv()

        def hand_over(s):
            return [pltpu.make_async_remote_copy(pool.at[hand_unit(s), :, pl.ds(c * cw, cw)], dr.at[s % ndr, :, pl.ds(c * cw, cw)],
                                                 dssem.at[s % 4, c], drsem.at[s, c],
                                                 device_id=place.partner(), device_id_type=MESH) for c in range(CHUNKS)]

        def stage_a(i, j):
            u = unit(ORDER2.index((i, j)))
            msg = ORDER2.index((j, i))
            for c in hand_over(msg):
                c.wait_recv()

            @pl.loop(0, block // 16)
            def _(r):
                rows = pl.ds(pl.multiple_of(r * 16, 16), 16)
                pool[u, rows, :] = (pool[u, rows, :].astype(f32) + dr[msg % ndr, rows, :].astype(f32)).astype(bf16)

            if msg + ndr < n_steps:
                pl.semaphore_signal(free.at[msg % ndr], inc=1, device_id=place.partner(), device_id_type=MESH)
            if j == 2:
                for c in copies(i, j):
                    c.start()

        def staged(i, j, p):
            if j == 0:
                return [pltpu.make_async_copy(m2_ref.at[i % SIDE, d], stage.at[p, d], st_sem.at[p, d]) for d in range(2)]
            d = 0 if j == 1 else 1
            return [pltpu.make_async_copy(m1_ref.at[i % SIDE, d], stage.at[p, 0, pl.ds(0, half)], st_sem.at[p, 0])]

        turn = {}

        def load_in(i, j):
            turn[(i, j)] = len(turn) % 2
            if j == 0:
                for d in range(2):
                    wait_in(m2_ref.at[i % SIDE, d], m2sem.at[i % SIDE, d])
            else:
                d = 0 if j == 1 else 1
                wait_in(m1_ref.at[i % SIDE, d], m1sem.at[i % SIDE, d])
            for c in staged(i, j, turn[(i, j)]):
                c.start()
            if j == 0 and i in (1, -1):
                d = 0 if i == 1 else 1
                wait_in(f1.at[d], f1sem.at[d])
            if j == 0 and i == 0:
                for d in range(2):
                    wait_in(f2.at[d], f2sem.at[d])

        def stage_b(i, j):
            p = turn[(i, j)]
            u = unit(ORDER2.index((i, j)))
            for c in staged(i, j, p):
                c.wait()
            if (i, j) == (0, 0):
                pltpu.make_async_copy(x_ref, xs, x_sem).wait()
            for h in range(2):
                if (j, h) in ((1, 1), (-1, 0)):
                    continue

                @pl.loop(0, half // 16)
                def _(r, h=h):
                    rows = pl.ds(pl.multiple_of(h * half + r * 16, 16), 16)
                    near = pl.ds(pl.multiple_of(r * 16, 16), 16)
                    total = pool[u, rows, :].astype(f32)
                    if j != 0:
                        total = total + stage[p, 0, near, :].astype(f32)
                    else:
                        total = total + stage[p, 0, rows, :].astype(f32) + stage[p, 1, rows, :].astype(f32)
                        if (i, h) == (1, 0):
                            total = total + f1[0, near, :].astype(f32)
                        if (i, h) == (-1, 1):
                            total = total + f1[1, near, :].astype(f32)
                        if i == 0:
                            total = total + f2[0, rows, :].astype(f32) + f2[1, rows, :].astype(f32)
                            total = xs[rows, :].astype(f32) + total.astype(bf16).astype(f32)
                    pool[u, rows, :] = total.astype(bf16)
            for c in copies(i, j):
                c.start()

        def serve(events):
            for kind, i, j in events:
                {"A": stage_a, "L": load_in, "B": stage_b}[kind](i, j)

        for c in step_loads(0):
            c.start()

        @pl.loop(0, n_steps)
        def _(step):
            for s in range(n_steps):
                @pl.when(step == s)
                def _(s=s):
                    serve(EVENTS2[s])
                    for c in step_loads(s):
                        c.wait()
                    if s + 1 < n_steps:
                        if s + 1 >= NS:
                            for c in copies(*ORDER2[s + 1 - NS]):
                                c.wait_send()
                        if s + 1 >= pool.shape[0] - NS:
                            for c in hand_over(s + 1 - (pool.shape[0] - NS)):
                                c.wait_send()
                        for c in step_loads(s + 1):
                            c.start()

            p = lax.rem(step, 2)
            b = place.chip(me, pick(step, [i for i, _ in ORDER2]), pick(step, [j for _, j in ORDER2]))
            scale = head ** -0.5 * LOG2E

            @pl.when(step >= 0)
            def _():
                m_sc[...] = jnp.full(m_sc.shape, NEG, f32)
                l_sc[...] = jnp.zeros(l_sc.shape, f32)
                acc_sc[...] = jnp.zeros(acc_sc.shape, f32)

            q_at = pl.ds(pl.multiple_of(b * pair, pair), pair)

            def attend(t, masked):
                rows = pl.ds(pl.multiple_of(t * KT, KT), KT)
                scores = []
                for g in range(2):
                    sc = jnp.dot(kk[rows, g * 128:(g + 1) * 128], qq[g * 128:(g + 1) * 128, q_at], preferred_element_type=f32)
                    if masked:
                        kp = t * KT + lax.broadcasted_iota(jnp.int32, (KT, pair), 0)
                        qp = b * pair + lax.broadcasted_iota(jnp.int32, (KT, pair), 1)
                        sc = jnp.where(kp <= qp, sc, NEG)
                    scores.append(sc)
                for g in range(2):
                    sc = scores[g]
                    old = m_sc[g:g + 1, :]
                    top = jnp.maximum(old, jnp.max(sc, axis=0, keepdims=True))
                    keep = jnp.exp2((old - top) * scale)
                    pr = jnp.exp2((sc - top) * scale)
                    l_sc[g:g + 1, :] = l_sc[g:g + 1, :] * keep + jnp.sum(pr, axis=0, keepdims=True)
                    acc_sc[g] = acc_sc[g] * keep + jnp.dot(vv[g * head:(g + 1) * head, rows], pr.astype(bf16),
                                                           preferred_element_type=f32)
                    m_sc[g:g + 1, :] = top

            full = lax.div(b, KT // pair)

            @pl.loop(0, full)
            def _(t):
                attend(t, False)

            @pl.when(step >= 0)
            def _():
                attend(full, True)
                for g in range(2):
                    o = acc_sc[g] / l_sc[g:g + 1, :]
                    lhs[p, :, pl.ds(ffl + g * head, head)] = o.T.astype(bf16)

            mine, theirs = lax.rem(step, NS), NS + lax.rem(step, pool.shape[0] - NS)
            low = mine * (1 - me) + theirs * me
            high = mine * me + theirs * (1 - me)
            is_early = functools.reduce(jnp.logical_or, [step == ORDER2.index(c) for c in EARLY]) if EARLY else step < 0

            @pl.when(is_early)
            def _():
                @pl.loop(0, CHUNKS)
                def _(c):
                    cols = col_chunk(c)
                    r = jnp.dot(lhs[p, :, ffl:ffl + hd2], w[ffl:ffl + hd2, cols], preferred_element_type=f32)
                    pool[low, :, cols] = (pool[low, :, cols].astype(f32) + r[:block]).astype(bf16)
                    pool[high, :, cols] = (pool[high, :, cols].astype(f32) + r[block:]).astype(bf16)

            @pl.when(jnp.logical_not(is_early))
            def _():
                @pl.loop(0, CHUNKS)
                def _(c):
                    cols = col_chunk(c)
                    r = jnp.dot(lhs[p, :, 0:ffl + hd2], w[:, cols], preferred_element_type=f32)
                    pool[low, :, cols] = r[:block].astype(bf16)
                    pool[high, :, cols] = r[block:].astype(bf16)

            for s in range(n_steps):
                @pl.when(step == s)
                def _(s=s):
                    if s >= ndr:
                        pl.semaphore_wait(free.at[s % ndr], 1)
                    for c in hand_over(s):
                        c.start()

        serve(EVENTS2[n_steps])
        out = pltpu.make_async_copy(pool.at[unit(ORDER2.index((0, 0)))], y_ref, x_sem)
        out.start()
        for s in range(n_steps - NS, n_steps):
            for c in copies(*ORDER2[s]):
                c.wait_send()
        for s in range(n_steps - (pool.shape[0] - NS), n_steps):
            for c in hand_over(s):
                c.wait_send()
        out.wait()

    pl.run_scoped(scatter, pltpu.VMEM((block, width), bf16), pltpu.VMEM((NS + 3, block, width), bf16),
                  pltpu.VMEM((2, 2, block, width), bf16),
                  pltpu.SemaphoreType.DMA, pltpu.SemaphoreType.DMA((2, 2)), pltpu.SemaphoreType.DMA((2, 2)))

    for n, (i, j, h) in enumerate(sends):
        if (i, j) != (0, 0):
            r = rows_of(me, i, j, h)
            pltpu.make_async_remote_copy(r, r, send.at[n], recv.at[0, 0, 0], device_id=place.partner(), device_id_type=MESH).wait_send()
    for i, j in STEPS[1:]:
        for h in range(2):
            r = rows_of(me, i, j, h)
            pltpu.make_async_remote_copy(r, r, dsend.at[i % SIDE, j % SIDE, h], recv.at[0, 0, 0],
                                         device_id=place.partner(), device_id_type=MESH).wait_send()


def layer(x, gain, bias, w_qkv, w_up, w_down, w_out, n_tp):
    block, width = x.shape
    seq = n_tp * block
    d, groups, three, head = w_qkv.shape
    wq = w_qkv.transpose(1, 2, 3, 0).reshape(groups * three * head, d)
    ffl = w_up.shape[1]
    hd2 = groups * head
    half = block // 2
    hbm = pl.BlockSpec(memory_space=pltpu.HBM)
    V, D, S = pltpu.VMEM, pltpu.SemaphoreType.DMA, jax.ShapeDtypeStruct
    return pl.pallas_call(
        layer_kernel,
        out_shape=(S((block, width), bf16), S((seq, width), bf16), S((seq, ffl), bf16), S((seq, width), bf16),
                   S((SIDE, 2, half, width), bf16), S((SIDE, 2, block, width), bf16)),
        in_specs=[hbm] * 7, out_specs=(hbm,) * 6,
        scratch_shapes=[
            V((ffl + hd2, width), bf16), V((groups * 128, seq), bf16), V((seq, groups * 128), bf16), V((hd2, seq), bf16),
            V((2, 2 * block, -(-(ffl + hd2) // 128) * 128), bf16), V((4, block, width), bf16),
            V((2, half, width), bf16), V((2, block, width), bf16),
            V((8, 2 * block), f32), V((8, 2 * block), f32), V((groups, head, 2 * block), f32),
            D((SIDE, SIDE, 2)), D((30,)), D((SIDE, SIDE, 2)), D((SIDE, SIDE, 2)),
            D((16, 2)), D((4, CHUNKS)), D((16, CHUNKS)), D((SIDE, 2)), D((SIDE, 2)), D((2,)), D((2,)),
            pltpu.SemaphoreType.REGULAR((4,)), D((2,))],
        compiler_params=pltpu.CompilerParams(collective_id=0, has_side_effects=True, vmem_limit_bytes=67043328),
        name="parallel_layer",
    )(x, gain.reshape(1, -1), bias.reshape(1, -1), wq, w_up, w_down, w_out)[0]


def solution(mesh):
    n_tp = mesh.shape["tp"]
    assert n_tp == 2 * SIDE * SIDE

    def local_layer(x_blk, ln_gain, ln_bias, w_qkv, w_out, w_up, w_down):
        x = x_blk.reshape(x_blk.shape[1:])
        return layer(x, ln_gain, ln_bias, w_qkv, w_up, w_down, w_out, n_tp)[None]

    return jax.shard_map(
        local_layer, mesh=mesh,
        in_specs=(P("dp", "tp", None), P(), P(), P(None, "tp", None, None),
                  P("tp", None), P(None, "tp"), P("tp", None)),
        out_specs=P("dp", "tp", None), check_vma=False)
```

time: 811 us -> 317 us (0.39); the launches traced: 799 us -> 317 us
  waiting for transfers between devices: 357 us -> 0 us
  matrix products: 325 us -> 0 us
  Pallas kernels: 0 us -> 314 us
  other arithmetic: 103 us -> 0 us
  between operations: 14 us -> 0.01 us
    pallas_call x0 -> x1, Pallas kernels: none -> 314 us  [layer(): pl.pallas_call(layer_kernel, out_shape=(S((block, width), bf16), S((seq,...]
    dot_general x5 -> x0, matrix products: 286 us -> none  [the longest x1 78.4 us: local_layer(): jnp.einsum('bsd,df->bsf', normed, w_up, preferred_element_type=jnp.float32)]
    reduce_scatter x1 -> x0, waiting for transfers between devices: 208 us -> none  [local_layer(): lax.psum_scatter(branch_part, 'tp', scatter_dimension=1, tiled=True)]
    all_gather x1 -> x0, waiting for transfers between devices: 148 us -> none  [local_layer(): x_full = lax.all_gather(x_blk, 'tp', axis=1, tiled=True)]
    reduce_sum x3 -> x0, other arithmetic: 82.2 us -> none  [the longest x1 46.2 us: local_layer(): attn_prob = jax.nn.softmax(scores, axis=-1).astype(jnp.bfloat16)]
    unnamed x1 -> x0, matrix products: 38.9 us -> none
    ge x1 -> x0, other arithmetic: 11 us -> none  [local_layer(): lax.broadcasted_iota(jnp.int32, (seq_len, seq_len), 0)]
    convert_element_type x2 -> x0, other arithmetic: 9.93 us -> none  [the longest x1 6.53 us: local_layer(): proj_qkv = jnp.einsum('bsd,dgjh->bsgjh', normed, w_qkv, preferred_element...]
  transfers between devices with their start and end apart: 2 -> 0, of which waited for: 2 -> 0; matrix products, arithmetic and copies ran while one was open for 1% -> 0% of each run, Pallas kernels for 0% -> 0%
where the time goes in v1:
time: 317 us
  Pallas kernels  314 us (99%)
    pallas_call x1, Pallas kernels, layer(): pl.pallas_call(layer_kernel, out_shape=(S((block, width), bf16), S((seq,...  314 us

profile of v1, /device:TPU:97, one launch (start us, length us, event | category | flops | bytes accessed | tf_op | source)
XLA Modules:
  0.0 316.9 jit_solution(18438392163691732011)
XLA Ops:
  0.0 314.2 %parallel_layer.1 = (bf16[128,6144]{1,0:T(8,128)(2,1)}, bf16[4096,6144]{1,0:T(8,128)(2,1)}, bf16[4096,768]{1,0:T(8,128)(2,1)}, bf16[4096,6144]{1,0:T(8,128)(2,1)...) custom-call(bf16[128,6144]{1,0:T(8,128)(2,1)} %bitcast.8, f32[1,6144]{1,0:T(1,128)} %bitcast.10, ...), custom_call_target="tpu_custom_call" | custom-call | tf_op jit(solution)/shard_map/parallel_layer/pallas_call | solution.py:595
  314.2 2.7 copy.9

commit v2 on v1

v2 whole, which is shorter than its diff:
```python
import functools

import jax
import jax.numpy as jnp
from jax import lax
from jax.experimental import pallas as pl
from jax.experimental.pallas import tpu as pltpu
from jax.sharding import PartitionSpec as P

OFFSETS = {"o": 0, "p": 1, "m": -1, "t": 2}


def place_of(text):
    return OFFSETS[text[0]], OFFSETS[text[1]]


def split(text, size):
    return [text[n:n + size] for n in range(0, len(text), size)]


def gather_events(text):
    return [("l", int(e[1:3])) if e[0] == "l" else (e[0],) + place_of(e[1:]) + (int(e[3]),) for e in split(text, 4)]


def scatter_events(text):
    return [(e[0],) + place_of(e[1:]) for e in split(text, 3)]


TILES = [
    "oo0oo1",
    "op0om1",
    "po0mo1",
    "op1om0",
    "po1mo0",
    "pp0mm1",
    "ot0ot1",
    "to0to1",
    "pm1mp0",
    "pm0mp1",
    "pt0mt1",
    "tp0tm1",
    "pt1mt0",
    "tp1tm0",
    "tt0tt1",
    "pp1mm0",
]
TILES = [[(place_of(u), int(u[2])) for u in split(text, 3)] for text in TILES]
BEFORE = [
    "aoo0aoo1Eoo1Eoo0Woo0Woo1Uoo1Uoo0Doo0Doo1l00-",
    "aop0aom1apo0amo1Emo1Wpo0Umo1Uom1Dpo0Dop0l01-l02-",
    "",
    "Upo0Dmo1aop1aom0apo1amo0l03-l04-",
    "",
    "Upo1Dmo0app0amm1ato0ato1l05-",
    "aot0aot1Uto1Dto0l06-",
    "apm0amp1",
    "apm1amp0l08-",
    "Upm1Dmp0l09-atp0atm1",
    "Utm1Dtp0apt0amt1l10-",
    "atp1atm0",
    "apt1amt0l12-",
    "att0att1",
    "",
    "l15-",
]
BEFORE = [gather_events(text) for text in BEFORE]
BETWEEN = [
    "",
    "",
    "",
    "",
    "",
    "",
    "Umm1Dpp0l07-",
    "Uto0Dto1",
    "",
    "",
    "Umo0Dpo1l11-",
    "",
    "l13-",
    "l14-",
    "app1amm0",
    "",
]
BETWEEN = [gather_events(text) for text in BETWEEN]
DOWNS = [0, 6, 7, 10, 11, 12, 13, 14]
EARLY = [place_of(text) for text in split("oootptmttotptmtt", 2)]
ORDER2 = [place_of(text) for text in split("tttppttmmtppmmpmmpottopoopmoomoo", 2)]
EVENTS2 = [
    "",
    "",
    "",
    "Apt",
    "Ltp",
    "Amt",
    "Btm",
    "Bpp",
    "Bmm",
    "AmpLmp",
    "Bpm",
    "AtoLto",
    "",
    "Aop",
    "",
    "Aom",
    "BpoBmoAooLomLopBomBopLooBoo",
]
EVENTS2 = [scatter_events(text) for text in EVENTS2]
MIDDLE2 = [
    "",
    "Att",
    "",
    "Atp",
    "Btp",
    "AtmLtm",
    "AppLpp",
    "AmmLmm",
    "",
    "BmpApmLpm",
    "",
    "BtoAot",
    "",
    "Apo",
    "",
    "LpoAmoLmo",
]
MIDDLE2 = [scatter_events(text) for text in MIDDLE2]
NS = 11
MESH = pl.DeviceIdType.MESH
SIDE = 4
LN_EPS = 1e-5
f32, bf16 = jnp.float32, jnp.bfloat16
KT = 1024
CHUNKS = 3
FINAL_STEPS = 2
NEG = -1e30
LOG2E = 1.4426950408889634


class Place:
    def __init__(self):
        self.tp = lax.axis_index("tp")
        self.colour = lax.rem(self.tp, 2)
        chip = lax.div(self.tp, 2)
        self.x, self.y = lax.rem(chip, SIDE), lax.div(chip, SIDE)

    def chip(self, colour, i, j):
        dx = (1 - colour) * i + colour * j
        dy = (1 - colour) * j + colour * i
        return lax.rem(self.y + dy + SIDE, SIDE) * SIDE + lax.rem(self.x + dx + SIDE, SIDE)

    def device(self, i, j):
        return {"tp": self.chip(self.colour, i, j) * 2 + self.colour}

    def partner(self):
        return {"tp": self.tp + 1 - 2 * self.colour}


def greet(place):
    barrier = pltpu.get_barrier_semaphore()
    others = [place.device(1, 0), place.device(-1, 0), place.device(0, 1), place.device(0, -1), place.partner()]
    for other in others:
        pl.semaphore_signal(barrier, inc=1, device_id=other, device_id_type=MESH)
    return lambda: pl.semaphore_wait(barrier, len(others))


ROUTES = {"W": (-1, 0), "E": (1, 0), "D": (0, -1), "U": (0, 1)}


def at_steps(step, count, body):
    for first in range(0, count, 4):
        @pl.when(jnp.logical_and(step >= first, step < first + 4))
        def _(first=first):
            for s in range(first, min(first + 4, count)):
                @pl.when(step == s)
                def _(s=s):
                    body(s)


def pick(step, values):
    r = jnp.int32(values[0])
    for n, v in enumerate(values[1:], 1):
        r = jnp.where(step == n, jnp.int32(v), r)
    return r


def layer_kernel(x_ref, gain_ref, bias_ref, wqkv_ref, wup_ref, wdown_ref, wout_ref,
                 p_ref, full_ref, act_ref, m_ref, m1_ref, m2_ref, f2,
                 w, qq, kk, vv, lhs, dr, f1, m_sc, l_sc, acc_sc,
                 recv, send, drecv, dsend, ssem, dssem, drsem, m1sem, m2sem, f1sem, f2sem, free, w_sem):
    place = Place()
    me = place.colour
    block, width = x_ref.shape
    half = block // 2
    ffl = wup_ref.shape[1]
    hd2 = wout_ref.shape[0]
    head = hd2 // 2
    pair = 2 * block
    n_steps = len(TILES)
    ndr = dr.shape[0]
    cw = width // CHUNKS

    wloads = [pltpu.make_async_copy(wdown_ref, w.at[pl.ds(0, ffl)], w_sem.at[0]),
              pltpu.make_async_copy(wout_ref, w.at[pl.ds(ffl, hd2)], w_sem.at[1])]

    def rows_of(colour, i, j, h):
        first = (place.chip(colour, i, j) * 2 + colour) * block + h * half
        return full_ref.at[pl.ds(pl.multiple_of(first, half), half)]

    def chip_rows(ref, i, j):
        return ref.at[pl.ds(pl.multiple_of(place.chip(me, i, j) * pair, pair), pair)]

    sent = [e for t in range(n_steps) for e in BEFORE[t] + BETWEEN[t] if e[0] in ROUTES]

    def stored(unit):
        (i, j), h = unit
        return pl.ds(pl.multiple_of(place.chip(me, i, j) * pair + h * block, block), block)

    def gather(xs, own, gain, bias, wqkv, wup, tile, acts, mst, in_sem, pw_sem, tile_sem, out_sem, mst_sem):
        loads = [pltpu.make_async_copy(x_ref, xs, in_sem.at[0]),
                 pltpu.make_async_copy(gain_ref, gain, in_sem.at[1]),
                 pltpu.make_async_copy(bias_ref, bias, in_sem.at[2])]
        pwloads = [pltpu.make_async_copy(wqkv_ref, wqkv, pw_sem.at[0]), pltpu.make_async_copy(wup_ref, wup, pw_sem.at[1])]
        for c in loads + pwloads + wloads:
            c.start()
        met = greet(place)
        for c in loads:
            c.wait()

        def norm_rows(start):
            g = gain[...]
            b = bias[...]

            @pl.loop(0, half // 16)
            def _(r):
                rows = pl.ds(pl.multiple_of(start + r * 16, 16), 16)
                v = xs[rows, :].astype(f32)
                mean = jnp.mean(v, axis=-1, keepdims=True)
                cen = v - mean
                var = jnp.mean(cen * cen, axis=-1, keepdims=True)
                own[rows, :] = (cen * lax.rsqrt(var + LN_EPS) * g + b).astype(bf16)

        def source(i, j, h):
            return own.at[pl.ds(h * half, half)] if (i, j) == (0, 0) else rows_of(me, i, j, h)

        def forward(kind, i, j, h):
            di, dj = ROUTES[kind]
            ri, rj = (i - di) % SIDE, (j - dj) % SIDE
            pltpu.make_async_remote_copy(source(i, j, h), rows_of(me, i, j, h), send.at[sent.index((kind, i, j, h))],
                                         recv.at[ri, rj, h], device_id=place.device(di, dj), device_id_type=MESH).start()

        def wait_block(colour, i, j, h, sem):
            r = rows_of(colour, i, j, h)
            pltpu.make_async_remote_copy(r, r, send.at[0], sem.at[i % SIDE, j % SIDE, h],
                                         device_id=place.partner(), device_id_type=MESH).wait_recv()

        def arrived(i, j, h):
            if (i, j) != (0, 0):
                wait_block(me, i, j, h, recv)
            pltpu.make_async_remote_copy(source(i, j, h), rows_of(me, i, j, h), dsend.at[i % SIDE, j % SIDE, h],
                                         drecv.at[i % SIDE, j % SIDE, h], device_id=place.partner(), device_id_type=MESH).start()

        def tile_parts(t, load):
            parts = []
            for u, ((i, j), h) in enumerate(TILES[t]):
                for n, colour in enumerate((me, 1 - me)):
                    if (i, j) == (0, 0) and n == 0:
                        if load:
                            tile[t % 2, pl.ds(pl.multiple_of(u * block + colour * half, half), half), :] = own[pl.ds(h * half, half), :]
                        continue
                    if load and n == 1:
                        wait_block(colour, j, i, h, drecv)
                    src = rows_of(me, i, j, h) if n == 0 else rows_of(colour, j, i, h)
                    parts.append(pltpu.make_async_copy(
                        src, tile.at[t % 2, pl.ds(pl.multiple_of(u * block + colour * half, half), half)],
                        tile_sem.at[t % 2, 2 * u + n]))
            return parts

        def act_out(t):
            return [pltpu.make_async_copy(acts.at[t % 2, pl.ds(u * block, block)], act_ref.at[stored(unit)], out_sem.at[t % 2, u])
                    for u, unit in enumerate(TILES[t]) if unit[0] not in EARLY]

        def m_out(t):
            return [pltpu.make_async_copy(mst.at[c, pl.ds(u * block, block)],
                                          m_ref.at[stored(unit), pl.ds(c * cw, cw)], mst_sem.at[c, u])
                    for c in range(CHUNKS) for u, unit in enumerate(TILES[t]) if unit[0] in EARLY]

        def serve(events):
            for e in events:
                if e[0] == "a":
                    arrived(*e[1:])
                elif e[0] == "l":
                    for c in tile_parts(e[1], True):
                        c.start()
                else:
                    forward(*e)

        norm_rows(0)
        norm_rows(half)
        met()
        serve([e for e in BEFORE[0] if e[0] != "l"])
        for g in range(2):
            qq[pl.ds(g * 128 + head, 128 - head), :] = jnp.zeros((128 - head, qq.shape[1]), bf16)

        @pl.loop(0, n_steps)
        def _(step):
            @functools.partial(at_steps, step, n_steps)
            def _(s):
                serve([e for e in BEFORE[s] if s or e[0] == "l"])
                if s >= 2:
                    for c in act_out(s - 2):
                        c.wait()
                if s == 0:
                    for c in pwloads:
                        c.wait()
                for c in tile_parts(s, False):
                    c.wait()

            p = lax.rem(step, 2)
            homes = []
            for u in range(2):
                units = [t[u] for t in TILES]
                b = place.chip(me, pick(step, [i for (i, _), _ in units]), pick(step, [j for (_, j), _ in units]))
                homes.append(pl.ds(pl.multiple_of(b * pair + pick(step, [h for _, h in units]) * block, block), block))

            @pl.when(step >= 0)
            def _():
                n = tile[p]
                qkv = lax.dot_general(wqkv[...], n, (((1,), (1,)), ((), ())), preferred_element_type=f32)
                for g in range(2):
                    base = g * 3 * head
                    keys = qkv[base + head:base + 2 * head]
                    keys = jnp.concatenate([keys, jnp.zeros((128 - head, pair), f32)], axis=0).T.astype(bf16)
                    for u in range(2):
                        cols = slice(u * block, (u + 1) * block)
                        qq[pl.ds(g * 128, head), homes[u]] = qkv[base:base + head, cols].astype(bf16)
                        kk[homes[u], pl.ds(g * 128, 128)] = keys[cols]
                        vv[pl.ds(g * head, head), homes[u]] = qkv[base + 2 * head:base + 3 * head, cols].astype(bf16)
                hid = jnp.dot(n, wup[...], preferred_element_type=f32)
                acts[p] = (0.5 * hid * (1.0 + lax.erf(hid * (0.5 ** 0.5)))).astype(bf16)

            @functools.partial(at_steps, step, n_steps)
            def _(s):
                serve(BETWEEN[s])
                for c in act_out(s):
                    c.start()
                if s in DOWNS:
                    if s == DOWNS[0]:
                        for c in wloads:
                            c.wait()
                    else:
                        for c in m_out(DOWNS[DOWNS.index(s) - 1]):
                            c.wait()

            @pl.when(functools.reduce(jnp.logical_or, [step == s for s in DOWNS]))
            def _():
                for c in range(CHUNKS):
                    mst[c] = jnp.dot(acts[p], w[0:ffl, c * cw:(c + 1) * cw], preferred_element_type=f32).astype(bf16)

            @functools.partial(at_steps, step, n_steps)
            def _(s):
                if s in DOWNS:
                    for c in m_out(s):
                        c.start()

        for s in (n_steps - 2, n_steps - 1):
            for c in act_out(s):
                c.wait()
        for c in m_out(DOWNS[-1]):
            c.wait()
        for n, (_, i, j, h) in enumerate(sent):
            if (i, j) == (0, 0):
                pltpu.make_async_remote_copy(source(0, 0, h), rows_of(me, 0, 0, h), send.at[n], recv.at[0, 0, 0],
                                             device_id=place.partner(), device_id_type=MESH).wait_send()
        for h in range(2):
            pltpu.make_async_remote_copy(source(0, 0, h), rows_of(me, 0, 0, h), dsend.at[0, 0, h], recv.at[0, 0, 0],
                                         device_id=place.partner(), device_id_type=MESH).wait_send()

    pl.run_scoped(
        gather, pltpu.VMEM((block, width), bf16), pltpu.VMEM((block, width), bf16), pltpu.VMEM((1, width), f32), pltpu.VMEM((1, width), f32),
        pltpu.VMEM(wqkv_ref.shape, bf16), pltpu.VMEM(wup_ref.shape, bf16), pltpu.VMEM((2, pair, width), bf16),
        pltpu.VMEM((2, pair, ffl), bf16), pltpu.VMEM((CHUNKS, pair, cw), bf16),
        pltpu.SemaphoreType.DMA((3,)), pltpu.SemaphoreType.DMA((2,)), pltpu.SemaphoreType.DMA((2, 4)), pltpu.SemaphoreType.DMA((2, 2)),
        pltpu.SemaphoreType.DMA((CHUNKS, 2)))

    def scatter(pool, stage, out_sem, lq_sem, st_sem):

        def unit(s):
            return s % NS

        def hand_unit(s):
            return NS + s % (pool.shape[0] - NS)

        def step_loads(s):
            i, j = ORDER2[s]
            base = place.chip(me, i, j) * pair
            if (i, j) in EARLY:
                res = []
                for n, (colour, u) in enumerate(((me, unit(s)), (1 - me, hand_unit(s)))):
                    for h in range(2):
                        at = pl.ds(pl.multiple_of(base + h * block + colour * half, half), half)
                        res.append(pltpu.make_async_copy(m_ref.at[at], pool.at[u, pl.ds(h * half, half)], lq_sem.at[s % 2, 2 * n + h]))
                return res
            return [pltpu.make_async_copy(chip_rows(act_ref, i, j), lhs.at[s % 2, :, pl.ds(0, ffl)], lq_sem.at[s % 2, 0])]

        def messages(i, j):
            if j == 2:
                return [(0, half, (0, 1), m1_ref.at[i % SIDE, 0], m1sem.at[i % SIDE, 0]),
                        (half, half, (0, -1), m1_ref.at[i % SIDE, 1], m1sem.at[i % SIDE, 1])]
            if j == 1:
                return [(0, block, (0, 1), m2_ref.at[i % SIDE, 0], m2sem.at[i % SIDE, 0])]
            if j == -1:
                return [(0, block, (0, -1), m2_ref.at[i % SIDE, 1], m2sem.at[i % SIDE, 1])]
            if i == 2:
                return [(0, half, (1, 0), f1.at[0], f1sem.at[0]), (half, half, (-1, 0), f1.at[1], f1sem.at[1])]
            if i == 1:
                return [(0, block, (1, 0), f2.at[0], f2sem.at[0])]
            if i == -1:
                return [(0, block, (-1, 0), f2.at[1], f2sem.at[1])]
            return []

        def copies(i, j):
            s = ORDER2.index((i, j))
            return [pltpu.make_async_remote_copy(pool.at[unit(s), pl.ds(r, n)], ref, ssem.at[s, m], sem,
                                                 device_id=place.device(*to), device_id_type=MESH)
                    for m, (r, n, to, ref, sem) in enumerate(messages(i, j))]

        def wait_in(ref, sem):
            pltpu.make_async_remote_copy(ref, ref, ssem.at[0, 0], sem, device_id=place.partner(), device_id_type=MESH).wait_recv()

        def hand_over(s):
            return [pltpu.make_async_remote_copy(pool.at[hand_unit(s), :, pl.ds(c * cw, cw)], dr.at[s % ndr, :, pl.ds(c * cw, cw)],
                                                 dssem.at[s % 4, c], drsem.at[s, c],
                                                 device_id=place.partner(), device_id_type=MESH) for c in range(CHUNKS)]

        def stage_a(i, j):
            u = unit(ORDER2.index((i, j)))
            msg = ORDER2.index((j, i))
            for c in hand_over(msg):
                c.wait_recv()

            @pl.loop(0, block // 32)
            def _(r):
                rows = pl.ds(pl.multiple_of(r * 32, 32), 32)
                pool[u, rows, :] = pool[u, rows, :] + dr[msg % ndr, rows, :]

            if msg + ndr < n_steps:
                pl.semaphore_signal(free.at[msg % ndr], inc=1, device_id=place.partner(), device_id_type=MESH)
            if j == 2:
                for c in copies(i, j):
                    c.start()
            if (i, j) == (0, 0):
                own_out(u).start()

        def own_out(u):
            return pltpu.make_async_copy(pool.at[u], p_ref, out_sem)

        def staged(i, j, p):
            if j == 0:
                return [pltpu.make_async_copy(m2_ref.at[i % SIDE, d], stage.at[p, d], st_sem.at[p, d]) for d in range(2)]
            d = 0 if j == 1 else 1
            return [pltpu.make_async_copy(m1_ref.at[i % SIDE, d], stage.at[p, 0, pl.ds(0, half)], st_sem.at[p, 0])]

        order = [e for s in range(n_steps + 1) for e in EVENTS2[s] + (MIDDLE2[s] if s < n_steps else [])]
        turn = {e[1:]: n % 2 for n, e in enumerate(e for e in order if e[0] == "L")}

        def load_in(i, j):
            if j == 0:
                for d in range(2):
                    wait_in(m2_ref.at[i % SIDE, d], m2sem.at[i % SIDE, d])
            else:
                d = 0 if j == 1 else 1
                wait_in(m1_ref.at[i % SIDE, d], m1sem.at[i % SIDE, d])
            for c in staged(i, j, turn[(i, j)]):
                c.start()
            if j == 0 and i in (1, -1):
                d = 0 if i == 1 else 1
                wait_in(f1.at[d], f1sem.at[d])

        def stage_b(i, j):
            p = turn[(i, j)]
            u = unit(ORDER2.index((i, j)))
            for c in staged(i, j, p):
                c.wait()
            for h in range(2):
                if (j, h) in ((1, 1), (-1, 0)):
                    continue

                @pl.loop(0, half // 16)
                def _(r, h=h):
                    rows = pl.ds(pl.multiple_of(h * half + r * 16, 16), 16)
                    near = pl.ds(pl.multiple_of(r * 16, 16), 16)
                    if j != 0:
                        pool[u, rows, :] = pool[u, rows, :] + stage[p, 0, near, :]
                    else:
                        total = pool[u, rows, :].astype(f32) + stage[p, 0, rows, :].astype(f32) + stage[p, 1, rows, :].astype(f32)
                        if (i, h) == (1, 0):
                            total = total + f1[0, near, :].astype(f32)
                        if (i, h) == (-1, 1):
                            total = total + f1[1, near, :].astype(f32)
                        pool[u, rows, :] = total.astype(bf16)
            for c in copies(i, j):
                c.start()

        def serve(events):
            for kind, i, j in events:
                if (kind, i, j) not in (("L", 0, 0), ("B", 0, 0)):
                    {"A": stage_a, "L": load_in, "B": stage_b}[kind](i, j)

        for c in step_loads(0):
            c.start()

        @pl.loop(0, n_steps)
        def _(step):
            @functools.partial(at_steps, step, n_steps)
            def _(s):
                serve(EVENTS2[s])
                if s + 1 < n_steps:
                    if s + 1 >= NS:
                        for c in copies(*ORDER2[s + 1 - NS]):
                            c.wait_send()
                    if s + 1 >= pool.shape[0] - NS:
                        for c in hand_over(s + 1 - (pool.shape[0] - NS)):
                            c.wait_send()
                    for c in step_loads(s + 1):
                        c.start()

            p = lax.rem(step, 2)
            b = place.chip(me, pick(step, [i for i, _ in ORDER2]), pick(step, [j for _, j in ORDER2]))
            scale = head ** -0.5 * LOG2E

            @pl.when(step >= 0)
            def _():
                m_sc[...] = jnp.full(m_sc.shape, NEG, f32)
                l_sc[...] = jnp.zeros(l_sc.shape, f32)
                acc_sc[...] = jnp.zeros(acc_sc.shape, f32)

            q_at = pl.ds(pl.multiple_of(b * pair, pair), pair)

            def position(at):
                return at % half + at // half % 2 * block + at // block * half

            def attend(t, width):
                size = width or KT
                rows = pl.ds(pl.multiple_of(t * KT, KT), size)
                scores = []
                for g in range(2):
                    sc = jnp.dot(kk[rows, g * 128:(g + 1) * 128], qq[g * 128:(g + 1) * 128, q_at], preferred_element_type=f32)
                    if width:
                        kp = position(lax.broadcasted_iota(jnp.int32, (pair, pair), 0))
                        qp = position(lax.broadcasted_iota(jnp.int32, (pair, pair), 1))
                        own = jnp.where(kp <= qp, sc[size - pair:], NEG)
                        sc = own if size == pair else jnp.concatenate([sc[:size - pair], own], axis=0)
                    scores.append(sc)
                for g in range(2):
                    sc = scores[g]
                    old = m_sc[g:g + 1, :]
                    top = jnp.maximum(old, jnp.max(sc, axis=0, keepdims=True))
                    keep = jnp.exp2((old - top) * scale)
                    pr = jnp.exp2((sc - top) * scale)
                    l_sc[g:g + 1, :] = l_sc[g:g + 1, :] * keep + jnp.sum(pr, axis=0, keepdims=True)
                    acc_sc[g] = acc_sc[g] * keep + jnp.dot(vv[g * head:(g + 1) * head, rows], pr.astype(bf16),
                                                           preferred_element_type=f32)
                    m_sc[g:g + 1, :] = top

            full = lax.div(b, KT // pair)

            @pl.loop(0, full)
            def _(t):
                attend(t, 0)

            for v in range(KT // pair):
                @pl.when(lax.rem(b, KT // pair) == v)
                def _(v=v):
                    attend(full, (v + 1) * pair)
                    for g in range(2):
                        o = acc_sc[g] / l_sc[g:g + 1, :]
                        lhs[p, :, pl.ds(ffl + g * head, head)] = o.T.astype(bf16)

            @functools.partial(at_steps, step, n_steps)
            def _(s):
                serve(MIDDLE2[s])
                for c in step_loads(s):
                    c.wait()

            mine, theirs = lax.rem(step, NS), NS + lax.rem(step, pool.shape[0] - NS)
            low = mine * (1 - me) + theirs * me
            high = mine * me + theirs * (1 - me)
            is_early = functools.reduce(jnp.logical_or, [step == ORDER2.index(c) for c in EARLY]) if EARLY else step < 0

            @pl.when(is_early)
            def _():
                for c in range(CHUNKS):
                    cols = slice(c * cw, (c + 1) * cw)
                    r = jnp.dot(lhs[p, :, ffl:ffl + hd2], w[ffl:ffl + hd2, cols], preferred_element_type=f32)
                    for h in range(2):
                        rows = slice(h * half, (h + 1) * half)
                        for u, first in ((low, h * block), (high, h * block + half)):
                            pool[u, rows, cols] = (pool[u, rows, cols].astype(f32) + r[first:first + half]).astype(bf16)

            @pl.when(jnp.logical_not(is_early))
            def _():
                for c in range(CHUNKS):
                    cols = slice(c * cw, (c + 1) * cw)
                    r = jnp.dot(lhs[p, :, 0:ffl + hd2], w[:, cols], preferred_element_type=f32)
                    for h in range(2):
                        rows = slice(h * half, (h + 1) * half)
                        for u, first in ((low, h * block), (high, h * block + half)):
                            pool[u, rows, cols] = r[first:first + half].astype(bf16)

            @functools.partial(at_steps, step, n_steps)
            def _(s):
                if s >= ndr:
                    pl.semaphore_wait(free.at[s % ndr], 1)
                for c in hand_over(s):
                    c.start()

        serve(EVENTS2[n_steps])
        for s in range(n_steps - NS, n_steps):
            for c in copies(*ORDER2[s]):
                c.wait_send()
        for s in range(n_steps - (pool.shape[0] - NS), n_steps):
            for c in hand_over(s):
                c.wait_send()
        own_out(unit(ORDER2.index((0, 0)))).wait()
        for d in range(2):
            wait_in(m2_ref.at[0, d], m2sem.at[0, d])
            wait_in(f2.at[d], f2sem.at[d])

    pl.run_scoped(scatter, pltpu.VMEM((NS + 3, block, width), bf16),
                  pltpu.VMEM((2, 2, block, width), bf16),
                  pltpu.SemaphoreType.DMA, pltpu.SemaphoreType.DMA((2, 4)), pltpu.SemaphoreType.DMA((2, 2)))

    for n, (_, i, j, h) in enumerate(sent):
        if (i, j) != (0, 0):
            r = rows_of(me, i, j, h)
            pltpu.make_async_remote_copy(r, r, send.at[n], recv.at[0, 0, 0], device_id=place.partner(), device_id_type=MESH).wait_send()
    for i, j in ORDER2[:-1]:
        for h in range(2):
            r = rows_of(me, i, j, h)
            pltpu.make_async_remote_copy(r, r, dsend.at[i % SIDE, j % SIDE, h], recv.at[0, 0, 0],
                                         device_id=place.partner(), device_id_type=MESH).wait_send()


def finish_kernel(x_ref, own_ref, second_ref, first_ref, y_ref):
    branch = own_ref[...].astype(f32)
    for part in (second_ref, first_ref):
        for d in range(2):
            branch = branch + part[d].astype(f32)
    y_ref[...] = (x_ref[...].astype(f32) + branch.astype(bf16).astype(f32)).astype(bf16)


def layer(x, gain, bias, w_qkv, w_up, w_down, w_out, n_tp):
    block, width = x.shape
    seq = n_tp * block
    d, groups, three, head = w_qkv.shape
    wq = w_qkv.transpose(1, 2, 3, 0).reshape(groups * three * head, d)
    ffl = w_up.shape[1]
    hd2 = groups * head
    half = block // 2
    hbm = pl.BlockSpec(memory_space=pltpu.HBM)
    V, D, S = pltpu.VMEM, pltpu.SemaphoreType.DMA, jax.ShapeDtypeStruct
    own, _, _, _, _, second, first = pl.pallas_call(
        layer_kernel,
        out_shape=(S((block, width), bf16), S((seq, width), bf16), S((seq, ffl), bf16), S((seq, width), bf16),
                   S((SIDE, 2, half, width), bf16), S((SIDE, 2, block, width), bf16), S((2, block, width), bf16)),
        in_specs=[hbm] * 7, out_specs=(hbm,) * 7,
        scratch_shapes=[
            V((ffl + hd2, width), bf16), V((groups * 128, seq), bf16), V((seq, groups * 128), bf16), V((hd2, seq), bf16),
            V((2, 2 * block, -(-(ffl + hd2) // 128) * 128), bf16), V((4, block, width), bf16),
            V((2, half, width), bf16),
            V((8, 2 * block), f32), V((8, 2 * block), f32), V((groups, head, 2 * block), f32),
            D((SIDE, SIDE, 2)), D((30,)), D((SIDE, SIDE, 2)), D((SIDE, SIDE, 2)),
            D((16, 2)), D((4, CHUNKS)), D((16, CHUNKS)), D((SIDE, 2)), D((SIDE, 2)), D((2,)), D((2,)),
            pltpu.SemaphoreType.REGULAR((4,)), D((2,))],
        compiler_params=pltpu.CompilerParams(collective_id=0, has_side_effects=True, vmem_limit_bytes=67043328),
        name="parallel_layer",
    )(x, gain.reshape(1, -1), bias.reshape(1, -1), wq, w_up, w_down, w_out)
    rows = block // FINAL_STEPS
    flat = pl.BlockSpec((rows, width), lambda n: (n, 0))
    return pl.pallas_call(
        finish_kernel,
        out_shape=S((block, width), bf16),
        grid=(FINAL_STEPS,),
        in_specs=[flat, flat, pl.BlockSpec((None, 2, rows, width), lambda n: (0, 0, n, 0)),
                  pl.BlockSpec((2, rows, width), lambda n: (0, n, 0))],
        out_specs=flat,
        name="finish",
    )(x, own, second, first)


def solution(mesh):
    n_tp = mesh.shape["tp"]
    assert n_tp == 2 * SIDE * SIDE

    def local_layer(x_blk, ln_gain, ln_bias, w_qkv, w_out, w_up, w_down):
        x = x_blk.reshape(x_blk.shape[1:])
        return layer(x, ln_gain, ln_bias, w_qkv, w_up, w_down, w_out, n_tp)[None]

    return jax.shard_map(
        local_layer, mesh=mesh,
        in_specs=(P("dp", "tp", None), P(), P(), P(None, "tp", None, None),
                  P("tp", None), P(None, "tp"), P("tp", None)),
        out_specs=P("dp", "tp", None), check_vma=False)
```

time: 317 us -> 300 us (0.946)
  Pallas kernels: 314 us -> 300 us
    pallas_call x1, Pallas kernels: 314 us -> 295 us  [layer(): pl.pallas_call(layer_kernel, out_shape=(S((block, width), bf16), S((seq,...]
    pallas_call x0 -> x1, Pallas kernels: none -> 5.32 us  [layer(): pl.pallas_call(finish_kernel, out_shape=S((block, width), bf16), grid=(FI...]
where the time goes in v2:
time: 300 us
  Pallas kernels  300 us (100%)
    pallas_call x1, Pallas kernels, layer(): pl.pallas_call(layer_kernel, out_shape=(S((block, width), bf16), S((seq,...  295 us

profile of v2, /device:TPU:97, one launch (start us, length us, event | category | flops | bytes accessed | tf_op | source)
XLA Modules:
  0.0 300.1 jit_solution(16567086517659496828)
XLA Ops:
  0.0 294.8 %parallel_layer.1 = (bf16[128,6144]{1,0:T(8,128)(2,1)}, bf16[4096,6144]{1,0:T(8,128)(2,1)}, bf16[4096,768]{1,0:T(8,128)(2,1)}, bf16[4096,6144]{1,0:T(8,128)(2,1)...) custom-call(bf16[128,6144]{1,0:T(8,128)(2,1)} %bitcast.8, ...), custom_call_target="tpu_custom_call" | custom-call | tf_op jit(solution)/shard_map/parallel_layer/pallas_call | solution.py:663
  294.8 5.3 %finish.1 = bf16[128,6144]{1,0:T(8,128)(2,1)} custom-call(bf16[128,6144]{1,0:T(8,128)(2,1)} %bitcast.9, bf16[128,6144]{1,0:T(8,128)(2,1)} %get-tuple-element.8.own_ref, bf16[4,2,128,6144]{3,2,1,0:T(8,128)(2,1)} %get-tuple-element.9.second_ref, bf16[2,128,6144]{2,1,0:T(8,128)(2,1)} %get-tuple-element.10.first_ref), custom_call_target="tpu_custom_call" | custom-call | tf_op jit(solution)/shard_map/finish/pallas_call | solution.py:681

commit v3 on v2

--- a/solution.py
+++ b/solution.py
@@ -60,8 +60,8 @@
     "atp1atm0",
     "apt1amt0l12-",
     "att0att1",
-    "",
-    "l15-",
+    "app1amm0",
+    "",
 ]
 BEFORE = [gather_events(text) for text in BEFORE]
 BETWEEN = [
@@ -79,7 +79,7 @@
     "",
     "l13-",
     "l14-",
-    "app1amm0",
+    "l15-",
     "",
 ]
 BETWEEN = [gather_events(text) for text in BETWEEN]

time: 300 us -> 298 us (level)
  Pallas kernels: 300 us -> 297 us
where the time goes in v3:
time: 298 us; the launch traced here: 297 us
  Pallas kernels  297 us (100%)
    pallas_call x1, Pallas kernels, layer(): pl.pallas_call(layer_kernel, out_shape=(S((block, width), bf16), S((seq,...  292 us

profile of v3, /device:TPU:97, one launch (start us, length us, event | category | flops | bytes accessed | tf_op | source)
XLA Modules:
  0.0 297.4 jit_solution(3774222807322544800)
XLA Ops:
  0.0 292.1 %parallel_layer.1 = (bf16[128,6144]{1,0:T(8,128)(2,1)}, bf16[4096,6144]{1,0:T(8,128)(2,1)}, bf16[4096,768]{1,0:T(8,128)(2,1)}, bf16[4096,6144]{1,0:T(8,128)(2,1)...) custom-call(bf16[128,6144]{1,0:T(8,128)(2,1)} %bitcast.8, ...), custom_call_target="tpu_custom_call" | custom-call | tf_op jit(solution)/shard_map/parallel_layer/pallas_call | solution.py:663
  292.1 5.3 %finish.1 = bf16[128,6144]{1,0:T(8,128)(2,1)} custom-call(bf16[128,6144]{1,0:T(8,128)(2,1)} %bitcast.9, bf16[128,6144]{1,0:T(8,128)(2,1)} %get-tuple-element.8.own_ref, bf16[4,2,128,6144]{3,2,1,0:T(8,128)(2,1)} %get-tuple-element.9.second_ref, bf16[2,128,6144]{2,1,0:T(8,128)(2,1)} %get-tuple-element.10.first_ref), custom_call_target="tpu_custom_call" | custom-call | tf_op jit(solution)/shard_map/finish/pallas_call | solution.py:681
